TPU v7x, 256 devices: a 4x2x16 block of a 4x16x16 slice. The times are simulated.
256 devices in a mesh: groups: 2 (over y), row: 16 (over z), col: 4 (over x), sub: 2 (over core).
Axes of the slice: x: 4, y: 2, z: 16, core: 2. Of those that a mesh axis runs over, the one named last changes fastest.
The devices are a block of a 4x16x16 slice.
Arguments:
- saved_alignment: bfloat16 [64, 1024, 256], P(('col', 'sub'), ('groups', 'row')), parts along dimension 1, may hold values from -6 to 6
- homolog_existence: int32 [64, 1024], P(('col', 'sub'), ('groups', 'row')), parts along dimension 1, may hold values 0 or 1
- amino_existence: int32 [1024], P(('groups', 'row')), parts along dimension 0, may hold values 0 or 1
- couple_delta_adjoint: bfloat16 [1024, 512, 128], P(('groups', 'row'), ('col', 'sub')), parts along dimension 0, may hold values from -1.5 to 1.5
- feedforward_adjoint: bfloat16 [64, 1024, 256], P(('col', 'sub'), ('groups', 'row')), parts along dimension 1, may hold values from -1.5 to 1.5
- feedforward_scale: float32 [256], replicated, may hold values from 0.1 to 1.9
- expansion_matrix: bfloat16 [256, 1024], replicated, may hold values from -0.375 to 0.375
- contraction_matrix: bfloat16 [1024, 256], replicated, may hold values from -0.1875 to 0.1875
- product_scale_vector: float32 [256], replicated, may hold values from 0.1 to 1.9
- twin_operand_matrix: bfloat16 [256, 64], replicated, may hold values from -0.375 to 0.375
- couple_projection_matrix: bfloat16 [1024, 128], replicated, may hold values from -0.1875 to 0.1875
Outputs:
- alignment_start_adjoint: bfloat16 [64, 1024, 256], P(('col', 'sub'), ('groups', 'row')), parts along dimension 1
- grad_out_weight: float32 [2048, 128], P('groups'), parts along dimension 0
- grad_factor_weight: float32 [512, 64], P('groups'), parts along dimension 0
- grad_w_in: float32 [512, 1024], P('groups'), parts along dimension 0
- grad_w_mid: float32 [2048, 256], P('groups'), parts along dimension 0
- feedforward_scale_adjoint: float32 [512], P('groups'), parts along dimension 0
- product_scale_adjoint: float32 [512], P('groups'), parts along dimension 0
There are 2 independent parts, one for each index of `groups`. A program takes and returns all parts, laid end to end along the dimension named above; an argument that names none is the same for every part. Nothing has to cross between parts.
All inputs are finite; a program needn't handle non-finite values. No bound on the sum of `homolog_existence` or of `amino_existence` on one device may be relied on, other than what follows from the above.
Results may differ from a plain program's by a relative error of at most 0.015.
Values may be sent and summed in bfloat16 or wider, within the bound.
No kernel may reach another device: no remote copies, remote signals or barrier semaphores. Data moves between devices by JAX's collectives and lax.ppermute only.
A program may use at most 64 MiB of HBM per device.

v0:
```python
import math
import jax
import jax.numpy as jnp
from jax import lax
from jax.sharding import PartitionSpec as P

epsilon = 1e-05


def in_one_piece(arrays, axis, dim, along):
    ends, at = ([], 0)
    for a in arrays[:-1]:
        at += a.shape[along]
        ends.append(at)
    both = jnp.concatenate(arrays, axis=along)
    return tuple(jnp.split(lax.all_gather(both, axis, axis=dim, tiled=True), ends, axis=along))


def joined_along(parts, dim):
    parts = jnp.moveaxis(parts, 0, dim)
    lengths = parts.shape
    return parts.reshape(*lengths[:dim], lengths[dim] * lengths[dim + 1], *lengths[dim + 2 :])


def one_gather(arrays, axis, dims):
    vector = jnp.concatenate([a.reshape(-1) for a in arrays])
    lines, at, done = (lax.all_gather(vector, axis), 0, [])
    for a, dim in zip(arrays, dims):
        parts = lines[:, at : at + a.size].reshape(-1, *a.shape)
        done.append(joined_along(parts, dim))
        at += a.size
    return tuple(done)


def split_up(shard, dim, devices):
    lengths = shard.shape
    parts = shard.reshape(*lengths[:dim], devices, lengths[dim] // devices, *lengths[dim + 1 :])
    return jnp.moveaxis(parts, dim, 0)


def sent_and_summed(shard, axis, dim):
    parts = split_up(shard, dim, lax.axis_size(axis))
    arrived = lax.all_to_all(parts, axis, split_axis=0, concat_axis=0, tiled=True)
    return arrived.astype(jnp.float32).sum(axis=0)


def layer_normalize(values):
    centre = jnp.mean(values, axis=-1, keepdims=True)
    centred = values - centre
    variance = jnp.mean(centred * centred, axis=-1, keepdims=True)
    inv_std = lax.rsqrt(variance + epsilon)
    return (centred * inv_std, inv_std)


def standardizer_adjoint(grad_hat, normed, inv_std):
    first_mean = jnp.mean(grad_hat, axis=-1, keepdims=True)
    second_mean = jnp.mean(grad_hat * normed, axis=-1, keepdims=True)
    return inv_std * (grad_hat - first_mean - normed * second_mean)


def exact_gelu(values):
    return jax.nn.gelu(values, approximate=False)


def contract_rows(first_arr, second_arr):
    return lax.dot_general(
        first_arr, second_arr, (((0,), (0,)), ((), ())), preferred_element_type=jnp.float32
    )


def contract_last(first_arr, second_arr):
    return lax.dot_general(
        first_arr, second_arr, (((1,), (1,)), ((), ())), preferred_element_type=jnp.float32
    )


def per_device(
    saved_alignment,
    homolog_existence,
    amino_existence,
    couple_delta_adjoint,
    feedforward_adjoint,
    feedforward_scale,
    expansion_matrix,
    contraction_matrix,
    product_scale_vector,
    twin_operand_matrix,
    couple_projection_matrix,
):
    homolog_split_total, amino_split_total, lane_breadth = saved_alignment.shape
    factor = twin_operand_matrix.shape[1] // 2
    pair_width = couple_projection_matrix.shape[1]
    existing_record_lines = homolog_split_total * amino_split_total
    shard_count = lax.axis_size(("col", "sub"))
    row_devices = lax.axis_size("row")
    total_res = amino_split_total * row_devices
    col_res = total_res // shard_count
    all_seqs = homolog_split_total * shard_count
    embedding_numbers = saved_alignment.astype(jnp.float32).reshape(
        existing_record_lines, lane_breadth
    )
    transition_standardized, transition_inv_deviation = layer_normalize(embedding_numbers)
    normalized_input = (transition_standardized * feedforward_scale).astype(jnp.bfloat16)
    hidden_pre = jnp.dot(normalized_input, expansion_matrix, preferred_element_type=jnp.float32)
    gelu_value, gelu_back = jax.vjp(exact_gelu, hidden_pre)
    hidden = gelu_value.astype(jnp.bfloat16)
    mixed_values = embedding_numbers + jnp.dot(
        hidden, contraction_matrix, preferred_element_type=jnp.float32
    )
    product_zscored, product_reciprocal_spread = layer_normalize(mixed_values)
    normalized_output = (product_zscored * product_scale_vector).astype(jnp.bfloat16)
    projected = jnp.dot(normalized_output, twin_operand_matrix, preferred_element_type=jnp.float32)
    keep_mask = (homolog_existence * amino_existence[None, :]).astype(jnp.float32)
    keep_col = keep_mask.reshape(existing_record_lines, 1)
    left_factor = (
        (projected[:, :factor] * keep_col)
        .astype(jnp.bfloat16)
        .reshape(homolog_split_total, amino_split_total * factor)
    )
    right_factor = (
        (projected[:, factor:] * keep_col)
        .astype(jnp.bfloat16)
        .reshape(homolog_split_total, amino_split_total * factor)
    )
    keep_half = keep_mask.astype(jnp.bfloat16)
    left_all, keep_rows = in_one_piece((left_factor, keep_half), ("col", "sub"), 0, 1)
    right_spread, keep_spread = one_gather((right_factor, keep_half), "row", (1, 1))
    right_flat, keep_cols = (
        lax.all_to_all(right_spread, ("col", "sub"), split_axis=1, concat_axis=0, tiled=True),
        lax.all_to_all(keep_spread, ("col", "sub"), split_axis=1, concat_axis=0, tiled=True),
    )
    right_cols = right_flat.reshape(all_seqs, col_res, factor)
    left_rows = left_all.reshape(all_seqs, amino_split_total, factor)
    pair_count = contract_rows(keep_rows, keep_cols)
    inverse = 1.0 / jnp.maximum(pair_count, 1.0)
    block_rows = math.gcd(amino_split_total, 16)
    result_adjoint = jnp.zeros((factor * factor, pair_width), jnp.float32)
    grad_right = jnp.zeros((all_seqs, col_res, factor), jnp.float32)
    left_parts = []
    for row_start in range(0, amino_split_total, block_rows):
        left_block = left_rows[:, row_start : row_start + block_rows, :]
        inv_block = inverse[row_start : row_start + block_rows]
        cot_block = couple_delta_adjoint[row_start : row_start + block_rows]
        outer_sum = jnp.einsum(
            "sip,sjq->ijpq", left_block, right_cols, preferred_element_type=jnp.float32
        )
        outer_half = (outer_sum * inv_block[:, :, None, None]).astype(jnp.bfloat16)
        outer_half = outer_half.reshape(block_rows, col_res, factor * factor)
        result_adjoint = result_adjoint + jnp.einsum(
            "ijk,ijl->kl", outer_half, cot_block, preferred_element_type=jnp.float32
        )
        pair_back = jnp.einsum(
            "ijl,kl->ijk", cot_block, couple_projection_matrix, preferred_element_type=jnp.float32
        )
        back_half = (pair_back * inv_block[:, :, None]).astype(jnp.bfloat16)
        back_half = back_half.reshape(block_rows, col_res, factor, factor)
        left_parts.append(
            jnp.einsum("ijpq,sjq->sip", back_half, right_cols, preferred_element_type=jnp.float32)
        )
        grad_right = grad_right + jnp.einsum(
            "ijpq,sip->sjq", back_half, left_block, preferred_element_type=jnp.float32
        )
    grad_left = jnp.concatenate(left_parts, axis=1).reshape(all_seqs, amino_split_total * factor)
    left_own = sent_and_summed(grad_left.astype(jnp.bfloat16), ("col", "sub"), 0)
    right_back = lax.all_to_all(
        grad_right.reshape(all_seqs, col_res * factor).astype(jnp.bfloat16),
        ("col", "sub"),
        split_axis=0,
        concat_axis=1,
        tiled=True,
    )
    right_own = sent_and_summed(right_back, "row", 1)
    grad_proj = jnp.concatenate(
        [
            left_own.reshape(existing_record_lines, factor),
            right_own.reshape(existing_record_lines, factor),
        ],
        axis=1,
    )
    grad_proj = (grad_proj * keep_col).astype(jnp.bfloat16)
    operand_adjoint = contract_rows(normalized_output, grad_proj)
    rescaled_result_adjoint = contract_last(grad_proj, twin_operand_matrix)
    product_scale_adjoint = jnp.sum(rescaled_result_adjoint * product_zscored, axis=0)
    combined_adjoint = feedforward_adjoint.astype(jnp.float32).reshape(
        existing_record_lines, lane_breadth
    ) + standardizer_adjoint(
        rescaled_result_adjoint * product_scale_vector, product_zscored, product_reciprocal_spread
    )
    grad_mixed_half = combined_adjoint.astype(jnp.bfloat16)
    hidden_adjoint = contract_rows(hidden, grad_mixed_half)
    grad_hidden = contract_last(grad_mixed_half, contraction_matrix)
    grad_pre = gelu_back(grad_hidden)[0].astype(jnp.bfloat16)
    expansion_adjoint = contract_rows(normalized_input, grad_pre)
    normed_input_gradient = contract_last(grad_pre, expansion_matrix)
    feedforward_scale_adjoint = jnp.sum(normed_input_gradient * transition_standardized, axis=0)
    alignment_start_adjoint = combined_adjoint + standardizer_adjoint(
        normed_input_gradient * feedforward_scale, transition_standardized, transition_inv_deviation
    )
    weight_grads = lax.psum(
        (
            result_adjoint,
            operand_adjoint,
            expansion_adjoint,
            hidden_adjoint,
            feedforward_scale_adjoint,
            product_scale_adjoint,
        ),
        ("row", "col", "sub"),
    )
    return (
        alignment_start_adjoint.astype(jnp.bfloat16).reshape(
            homolog_split_total, amino_split_total, lane_breadth
        ),
        weight_grads[0],
        weight_grads[1],
        weight_grads[2],
        weight_grads[3],
        weight_grads[4],
        weight_grads[5],
    )


def solution(mesh):
    return jax.shard_map(
        per_device,
        mesh=mesh,
        in_specs=(
            P(("col", "sub"), ("groups", "row"), None),
            P(("col", "sub"), ("groups", "row")),
            P(("groups", "row")),
            P(("groups", "row"), ("col", "sub"), None),
            P(("col", "sub"), ("groups", "row"), None),
            P(),
            P(),
            P(),
            P(),
            P(),
            P(),
        ),
        out_specs=(
            P(("col", "sub"), ("groups", "row"), None),
            P("groups", None),
            P("groups", None),
            P("groups", None),
            P("groups", None),
            P("groups"),
            P("groups"),
        ),
        check_vma=False,
    )
```

profile of v0, /device:TPU:33, one launch (start us, length us, event | category | flops | bytes accessed | tf_op | source)
XLA Modules:
  0.0 527.1 jit_solution(18394093957308587515)
XLA Ops:
  7.2 1.1 convert_reduce_fusion.2
  8.4 1.1 multiply_reduce_fusion.5
  9.5 0.7 fusion.61
  10.4 1.0 multiply_convert_fusion.4
  11.5 3.4 multiply_convert_fusion.2
  15.0 0.8 copy-done.5
  15.8 0.4 fusion.63
  16.2 0.2 multiply_reduce_fusion.4
  16.4 0.4 copy-done.13
  16.8 0.1 multiply_convert_fusion.3
  16.9 0.2 fusion.65
  17.4 45.3 %all-gather.1 = bf16[16,1,8448]{2,1,0:T(2,128)(2,1)S(1)} all-gather(bf16[1,1,8448]{2,1,0:T(2,128)(2,1)S(1)} %reshape.176), channel_id=2, replica_groups=mesh['groups'=2,'row'=16,'col'=4,'sub'=2] {'row'}, dimensions={0}, use_global_device_ids=true | all-gather | bytes 287232 | tf_op jit(solution)/shard_map/all_gather | solution.py:27
  62.9 0.7 reshape.192
  63.6 12.2 %all-to-all-start.1 = ((bf16[8,2,256]{2,1,0:T(2,128)(2,1)}), bf16[8,2,256]{2,1,0:T(2,128)(2,1)S(1)}, u32[]{:S(2)}, u32[]{:S(2)}) async-start(bf16[8,2,256]{2,1,0:T(2,128)(2,1)} %reshape.192), calls=%async_computation.1 | async-start | bytes 16384 | tf_op jit(solution)/shard_map/all_to_all | solution.py:130
  76.1 13.7 %all_gather.11 = bf16[64,1056]{1,0:T(8,128)(2,1)S(1)} all-gather(bf16[8,1056]{1,0:T(8,128)(2,1)S(1)} %pad_maximum_fusion.2), channel_id=1, replica_groups=mesh['groups'=2,'row'=16,'col'=4,'sub'=2] {'col','sub'}, dimensions={0}, use_global_device_ids=true | all-gather | bytes 152064 | tf_op jit(solution)/shard_map/all_gather | solution.py:16
  89.8 0.2 copy.60
  90.1 0.9 copy.49
  90.9 4.1 all-to-all-start
  95.1 0.2 fusion.35
  95.3 1.7 multiply_convert_fusion
  97.1 3.2 copy.56
  100.3 1.7 multiply_convert_fusion.1
  102.0 3.2 copy.53
  105.2 3.8 fusion.10
  109.0 1.5 fusion.19
  110.5 0.8 copy.63
  111.2 1.8 convert_element_type.80
  113.1 5.0 all-to-all-start.3
  118.1 1.9 reshape.161
  120.0 1.0 copy.54
  120.9 3.6 fusion.29
  124.6 1.3 fusion.32
  125.9 1.0 copy.76
  126.9 0.8 copy.59
  127.7 1.2 convert_element_type.77
  128.9 4.8 all-to-all-start.2
  133.7 3.2 fusion.1
  136.9 0.1 copy.64
  137.2 0.9 copy.65
  138.0 1.0 all-to-all-done.2
  139.0 4.0 all-to-all-start.4
  143.0 0.3 all-reduce.4.cloned.1.call-start
  143.3 1.2 fusion
  144.5 0.9 copy-done.3
  145.4 2.7 copy.67
  148.2 2.7 copy.70
  150.9 0.9 convolution_bitcast_fusion
  151.9 1.8 fusion.22
  153.8 2.7 all-to-all-done.4
  156.7 0.1 fusion.49
  156.8 0.8 fusion.66
  157.6 0.3 multiply_reduce_fusion
  158.0 0.2 convert_add_fusion
  158.2 1.3 fusion.50
  159.6 2.1 add_convert_fusion
  161.7 1.3 fusion.67
  163.1 0.5 multiply_reduce_fusion.1
  163.6 252.7 %all-reduce = (f32[256]{0:T(256)}, f32[256]{0:T(256)}) all-reduce(f32[256]{0:T(256)S(1)} %get-tuple-element.9, f32[256]{0:T(256)S(1)} %get-tuple-element.7), channel_id=1, replica_groups=mesh['groups'=2,'row'=16,'col'=4,'sub'=2] {'row','col','sub'}, use_global_device_ids=true, to_apply=%region_15.0 | all-reduce | flops 512 | bytes 4096 | tf_op jit(solution)/shard_map/psum | solution.py:199
  416.2 0.9 add_convert_fusion.1
  417.1 95.3 %all-reduce.4.cloned.1.call-done = (f32[1024,128]{1,0:T(8,128)}, f32[256,64]{0,1:T(8,128)}, f32[256,1024]{1,0:T(8,128)}, f32[1024,256]{1,0:T(8,128)}) async-done(((f32[1024,128]{1,0:T(8,128)}, f32[256,64]{0,1:T(8,128)}, f32[256,1024]{1,0:T(8,128)}, f32[1024,256]{1,0:T(8,128)}), (f32[1024,128]{1,0:T(8,128)}, f32[256,64]{0,1:T(8,128)}, f32[256,1024]{1,0:T(8,128)}, ...) | async-done | bytes 2686992 | tf_op jit(solution)/shard_map/psum | solution.py:199
  512.4 1.9 copy.122
  514.2 1.5 copy.123
  515.7 2.3 copy.124
  518.0 2.3 copy.125
  (90 shorter events, 1.9 us)
Async XLA Ops:
  7.2 4.3 copy-start
  8.4 6.6 %copy-start.17 = (f32[256]{0:T(256)}, f32[256]{0:T(256)S(1)}, u32[]{:S(2)}) copy-start(f32[256]{0:T(256)S(1)} %div.30) | copy-start | bytes 3076
  9.5 5.4 %copy-start.19 = (f32[256]{0:T(256)}, f32[256]{0:T(256)S(1)}, u32[]{:S(2)}) copy-start(f32[256]{0:T(256)S(1)} %rsqrt.20) | copy-start | bytes 3076
  10.3 6.7 %copy-start.21 = (f32[256]{0:T(256)}, f32[256]{0:T(256)S(1)}, u32[]{:S(2)}) copy-start(f32[256]{0:T(256)S(1)} %mul.200) | copy-start | bytes 3076
  11.5 4.3 copy-start.4
  11.5 4.3 copy-start.8
  11.5 5.3 copy-start.23
  11.5 5.4 %copy-start.10 = (bf16[256,64]{0,1:T(8,128)(2,1)S(1)}, bf16[256,64]{0,1:T(8,128)(2,1)}, u32[]{:S(2)}) copy-start(bf16[256,64]{0,1:T(8,128)(2,1)} %param.20) | copy-start | bytes 98308
  15.0 0.8 copy-start.5
  16.2 0.6 copy-start.13
  16.8 59.3 %copy-start.15 = (f32[256]{0:T(256)}, f32[256]{0:T(256)S(1)}, u32[]{:S(2)}) copy-start(f32[256]{0:T(256)S(1)} %add_rsqrt_fusion.1) | copy-start | bytes 3076
  63.6 27.3 %all-to-all-start.1 = ((bf16[8,2,256]{2,1,0:T(2,128)(2,1)}), bf16[8,2,256]{2,1,0:T(2,128)(2,1)S(1)}, u32[]{:S(2)}, u32[]{:S(2)}) async-start(bf16[8,2,256]{2,1,0:T(2,128)(2,1)} %reshape.192), calls=%async_computation.1 | async-start | bytes 16384 | tf_op jit(solution)/shard_map/all_to_all | solution.py:130
  90.9 22.1 %all-to-all-start = ((bf16[8,8,2048]{2,0,1:T(8,128)(2,1)}), bf16[8,8,2048]{2,0,1:T(8,128)(2,1)}, u32[]{:S(2)}, u32[]{:S(2)}) async-start(bf16[8,8,2048]{2,0,1:T(8,128)(2,1)} %copy.49), calls=%async_computation | async-start | bytes 524288 | tf_op jit(solution)/shard_map/all_to_all | solution.py:129
  105.2 3.8 copy-start.1
  113.1 15.9 %all-to-all-start.3 = ((bf16[8,8,2048]{2,1,0:T(8,128)(2,1)}), bf16[8,8,2048]{2,1,0:T(8,128)(2,1)S(1)}, u32[]{:S(2)}, u32[]{:S(2)}) async-start(bf16[8,8,2048]{2,1,0:T(8,128)(2,1)} %convert_element_type.80), calls=%async_computation.3 | async-start | bytes 524288 | tf_op jit(solution)/shard_map/all_to_all | solution.py:165
  120.9 3.7 copy-start.2
  128.9 10.1 %all-to-all-start.2 = ((bf16[8,8,1024]{2,1,0:T(8,128)(2,1)}), bf16[8,8,1024]{2,1,0:T(8,128)(2,1)S(1)}, u32[]{:S(2)}, u32[]{:S(2)}) async-start(bf16[8,8,1024]{2,1,0:T(8,128)(2,1)} %convert_element_type.77), calls=%async_computation.2 | async-start | bytes 262144 | tf_op jit(solution)/shard_map/all_to_all | solution.py:43
  139.0 17.5 %all-to-all-start.4 = ((bf16[16,8,1024]{2,1,0:T(8,128)(2,1)}), bf16[16,8,1024]{2,1,0:T(8,128)(2,1)S(1)}, u32[]{:S(2)}, u32[]{:S(2)}) async-start(bf16[16,8,1024]{2,1,0:T(8,128)(2,1)} %copy.65), calls=%async_computation.4 | async-start | bytes 524288 | tf_op jit(solution)/shard_map/all_to_all | solution.py:43
  143.0 369.4 %all-reduce.4.cloned.1.call-start = ((), (), s32[]{:S(2)}) async-start(), calls=%async_computation.5 | async-start | bytes 5373952 | tf_op jit(solution)/shard_map/psum | solution.py:199
  143.3 2.2 copy-start.3
  148.1 2.7 copy-start.7
  151.8 4.8 copy-start.22
  151.8 5.8 %copy-start.11 = (bf16[256,64]{0,1:T(8,128)(2,1)S(1)}, bf16[256,64]{0,1:T(8,128)(2,1)}, u32[]{:S(2)}) copy-start(bf16[256,64]{0,1:T(8,128)(2,1)} %param.20) | copy-start | bytes 98308
  151.8 5.8 %copy-start.14 = (f32[256]{0:T(256)S(1)}, f32[256]{0:T(256)}, u32[]{:S(2)}) copy-start(f32[256]{0:T(256)} %copy-done.13) | copy-start | bytes 3076
  151.8 5.8 %copy-start.16 = (f32[256]{0:T(256)S(1)}, f32[256]{0:T(256)}, u32[]{:S(2)}) copy-start(f32[256]{0:T(256)} %copy-done.15) | copy-start | bytes 3076
  151.9 5.8 %copy-start.24 = (f32[256]{0:T(256)S(1)}, f32[256]{0:T(256)}, u32[]{:S(2)}) copy-start(f32[256]{0:T(256)} %param.19) | copy-start | bytes 3076
  151.9 6.1 %copy-start.12 = (bf16[8,32,256]{2,1,0:T(8,128)(2,1)S(1)}, bf16[8,32,256]{2,1,0:T(8,128)(2,1)}, u32[]{:S(2)}) copy-start(bf16[8,32,256]{2,1,0:T(8,128)(2,1)} %param.15) | copy-start | bytes 393220
  151.9 6.3 %copy-start.6 = (bf16[256,1024]{1,0:T(8,128)(2,1)S(1)}, bf16[256,1024]{1,0:T(8,128)(2,1)}, u32[]{:S(2)}) copy-start(bf16[256,1024]{1,0:T(8,128)(2,1)} %copy-done.5) | copy-start | bytes 1572868
  151.9 7.7 %copy-start.9 = (bf16[1024,256]{1,0:T(8,128)(2,1)S(1)}, bf16[1024,256]{1,0:T(8,128)(2,1)}, u32[]{:S(2)}) copy-start(bf16[1024,256]{1,0:T(8,128)(2,1)} %param.18) | copy-start | bytes 1572868
  159.5 3.5 copy-start.18
  159.5 3.5 copy-start.20
  159.5 3.5 copy-start.25
Sparse Core Ops, SparseCore 0:
  163.2 349.1 all-reduce.3
where the time goes:
time: 528 us; the launch traced here: 527 us
  blocking collectives  312 us (59%)
  waiting for transfers between devices  99 us (19%)
  local copies, waits for them, and re-layouts  34.5 us (7%)
  matrix products  31.3 us (6%)
  starting transfers between devices  30.4 us (6%)
  between operations  14.6 us (3%)
  other arithmetic  5.63 us (1%)
    psum x1, blocking collectives, per_device(): lax.psum((result_adjoint, operand_adjoint, expansion_adjoint, hidden_adjo...  253 us
    psum x1, waiting for transfers between devices, per_device(): lax.psum((result_adjoint, operand_adjoint, expansion_adjoint, hidden_adjo...  95.3 us
    all_gather x1, blocking collectives, one_gather(): lines, at, done = (lax.all_gather(vector, axis), 0, [])  45.3 us
    all_gather x1, blocking collectives, in_one_piece(): lax.all_gather(both, axis, axis=dim, tiled=True)  13.7 us
    all_to_all x1, starting transfers between devices, per_device(): lax.all_to_all(keep_spread, ('col', 'sub'), split_axis=1, concat_axis=0,...  12.2 us
    unnamed x60, local copies, waits for them, and re-layouts  11 us
  transfers between devices with their start and end apart: 6, of which 3 were waited for; matrix products, arithmetic and copies ran while one was open for 9% of the time, Pallas kernels for 0%

commit v1 on v0

--- a/solution.py
+++ b/solution.py
@@ -197,15 +197,18 @@
         normed_input_gradient * feedforward_scale, transition_standardized, transition_inv_deviation
     )
     weight_grads = lax.psum(
-        (
-            result_adjoint,
-            operand_adjoint,
-            expansion_adjoint,
-            hidden_adjoint,
-            feedforward_scale_adjoint,
-            product_scale_adjoint,
-        ),
-        ("row", "col", "sub"),
+        lax.psum(
+            (
+                result_adjoint,
+                operand_adjoint,
+                expansion_adjoint,
+                hidden_adjoint,
+                feedforward_scale_adjoint,
+                product_scale_adjoint,
+            ),
+            "row",
+        ),
+        ("col", "sub"),
     )
     return (
         alignment_start_adjoint.astype(jnp.bfloat16).reshape(

time: 528 us -> 401 us (0.76)
  blocking collectives: 312 us -> 109 us
  waiting for transfers between devices: 99 us -> 173 us
    psum x1, blocking collectives: 253 us -> 21 us  [per_device(): lax.psum((result_adjoint, operand_adjoint, expansion_adjoint, hidden_adjo...]
    psum x1, waiting for transfers between devices: 95.3 us -> 136 us  [per_device(): lax.psum((result_adjoint, operand_adjoint, expansion_adjoint, hidden_adjo...]
    psum x0 -> x1, waiting for transfers between devices: none -> 33.9 us  [per_device(): lax.psum(lax.psum((result_adjoint, operand_adjoint, expansion_adjoint, hi...]
    psum x0 -> x1, blocking collectives: none -> 29.3 us  [per_device(): lax.psum(lax.psum((result_adjoint, operand_adjoint, expansion_adjoint, hi...]
  transfers between devices with their start and end apart: 6 -> 7, of which waited for: 3 -> 4; matrix products, arithmetic and copies ran while one was open for 9% -> 11% of each run, Pallas kernels for 0% -> 0%
where the time goes in v1:
time: 401 us; the launch traced here: 400 us
  waiting for transfers between devices  173 us (43%)
  blocking collectives  109 us (27%)
  local copies, waits for them, and re-layouts  35.1 us (9%)
  matrix products  31.3 us (8%)
  starting transfers between devices  30.5 us (8%)
  between operations  14.6 us (4%)
  other arithmetic  5.63 us (1%)
    psum x1, waiting for transfers between devices, per_device(): lax.psum((result_adjoint, operand_adjoint, expansion_adjoint, hidden_adjo...  136 us
    all_gather x1, blocking collectives, one_gather(): lines, at, done = (lax.all_gather(vector, axis), 0, [])  45.3 us
    psum x1, waiting for transfers between devices, per_device(): lax.psum(lax.psum((result_adjoint, operand_adjoint, expansion_adjoint, hi...  33.9 us
    psum x1, blocking collectives, per_device(): lax.psum(lax.psum((result_adjoint, operand_adjoint, expansion_adjoint, hi...  29.3 us
    psum x1, blocking collectives, per_device(): lax.psum((result_adjoint, operand_adjoint, expansion_adjoint, hidden_adjo...  21 us
    all_gather x1, blocking collectives, in_one_piece(): lax.all_gather(both, axis, axis=dim, tiled=True)  13.7 us
    all_to_all x1, starting transfers between devices, per_device(): lax.all_to_all(keep_spread, ('col', 'sub'), split_axis=1, concat_axis=0,...  12.2 us
    unnamed x60, local copies, waits for them, and re-layouts  11.6 us
  transfers between devices with their start and end apart: 7, of which 4 were waited for; matrix products, arithmetic and copies ran while one was open for 11% of the time, Pallas kernels for 0%

profile of v1, /device:TPU:33, one launch (start us, length us, event | category | flops | bytes accessed | tf_op | source)
XLA Modules:
  0.0 399.7 jit_solution(12549568316085416656)
XLA Ops:
  7.2 1.1 convert_reduce_fusion.2
  8.4 1.1 multiply_reduce_fusion.5
  9.5 0.7 fusion.61
  10.4 1.0 multiply_convert_fusion.4
  11.5 3.4 multiply_convert_fusion.2
  15.0 0.8 copy-done.5
  15.8 0.4 fusion.63
  16.2 0.2 multiply_reduce_fusion.4
  16.4 0.4 copy-done.13
  16.8 0.6 copy-done.15
  17.5 0.2 fusion.65
  17.9 45.3 %all-gather.1 = bf16[16,1,8448]{2,1,0:T(2,128)(2,1)S(1)} all-gather(bf16[1,1,8448]{2,1,0:T(2,128)(2,1)S(1)} %reshape.176), channel_id=2, replica_groups=mesh['groups'=2,'row'=16,'col'=4,'sub'=2] {'row'}, dimensions={0}, use_global_device_ids=true | all-gather | bytes 287232 | tf_op jit(solution)/shard_map/all_gather | solution.py:27
  63.5 0.7 reshape.192
  64.2 12.2 %all-to-all-start.1 = ((bf16[8,2,256]{2,1,0:T(2,128)(2,1)}), bf16[8,2,256]{2,1,0:T(2,128)(2,1)S(1)}, u32[]{:S(2)}, u32[]{:S(2)}) async-start(bf16[8,2,256]{2,1,0:T(2,128)(2,1)} %reshape.192), calls=%async_computation.1 | async-start | bytes 16384 | tf_op jit(solution)/shard_map/all_to_all | solution.py:130
  76.6 13.7 %all_gather.11 = bf16[64,1056]{1,0:T(8,128)(2,1)S(1)} all-gather(bf16[8,1056]{1,0:T(8,128)(2,1)S(1)} %pad_maximum_fusion.2), channel_id=1, replica_groups=mesh['groups'=2,'row'=16,'col'=4,'sub'=2] {'col','sub'}, dimensions={0}, use_global_device_ids=true | all-gather | bytes 152064 | tf_op jit(solution)/shard_map/all_gather | solution.py:16
  90.3 0.2 copy.60
  90.6 0.9 copy.49
  91.5 4.1 %all-to-all-start = ((bf16[8,8,2048]{2,0,1:T(8,128)(2,1)}), bf16[8,8,2048]{2,0,1:T(8,128)(2,1)}, u32[]{:S(2)}, u32[]{:S(2)}) async-start(bf16[8,8,2048]{2,0,1:T(8,128)(2,1)} %copy.49), calls=%async_computation | async-start | bytes 524288 | tf_op jit(solution)/shard_map/all_to_all | solution.py:129
  95.7 0.2 fusion.35
  95.9 1.8 multiply_convert_fusion
  97.6 3.2 copy.56
  100.8 1.7 multiply_convert_fusion.1
  102.6 3.2 copy.53
  105.7 3.8 fusion.10
  109.5 1.5 fusion.19
  111.0 0.8 copy.63
  111.8 1.8 convert_element_type.80
  113.6 5.0 %all-to-all-start.3 = ((bf16[8,8,2048]{2,1,0:T(8,128)(2,1)}), bf16[8,8,2048]{2,1,0:T(8,128)(2,1)S(1)}, u32[]{:S(2)}, u32[]{:S(2)}) async-start(bf16[8,8,2048]{2,1,0:T(8,128)(2,1)} %convert_element_type.80), calls=%async_computation.3 | async-start | bytes 524288 | tf_op jit(solution)/shard_map/all_to_all | solution.py:165
  118.7 1.9 reshape.161
  120.5 1.0 copy.54
  121.5 3.6 fusion.29
  125.1 1.3 fusion.32
  126.5 1.0 copy.76
  127.5 0.8 copy.59
  128.3 1.2 convert_element_type.77
  129.5 4.8 %all-to-all-start.2 = ((bf16[8,8,1024]{2,1,0:T(8,128)(2,1)}), bf16[8,8,1024]{2,1,0:T(8,128)(2,1)S(1)}, u32[]{:S(2)}, u32[]{:S(2)}) async-start(bf16[8,8,1024]{2,1,0:T(8,128)(2,1)} %convert_element_type.77), calls=%async_computation.2 | async-start | bytes 262144 | tf_op jit(solution)/shard_map/all_to_all | solution.py:43
  134.3 3.2 fusion.1
  137.7 0.9 copy.65
  138.6 1.0 all-to-all-done.2
  139.5 4.0 all-to-all-start.4
  143.5 0.3 all-reduce.7.cloned.1.call-start
  143.8 1.2 fusion
  145.1 0.9 copy-done.3
  146.0 2.7 copy.67
  148.7 2.7 copy.70
  151.4 0.9 convolution_bitcast_fusion
  152.5 1.8 fusion.22
  154.3 2.7 all-to-all-done.4
  157.3 0.8 fusion.66
  158.2 0.3 multiply_reduce_fusion
  158.5 0.2 convert_add_fusion
  158.8 1.3 fusion.50
  160.1 2.1 add_convert_fusion
  162.3 1.3 fusion.67
  163.7 135.6 %all-reduce.7.cloned.1.call-done = (f32[1024,128]{1,0:T(8,128)}, f32[256,64]{0,1:T(8,128)}, f32[256,1024]{1,0:T(8,128)}, f32[1024,256]{1,0:T(8,128)}) async-done(((f32[1024,128]{1,0:T(8,128)}, f32[256,64]{0,1:T(8,128)}, f32[256,1024]{1,0:T(8,128)}, f32[1024,256]{1,0:T(8,128)}), (f32[1024,128]{1,0:T(8,128)}, f32[256,64]{0,1:T(8,128)}, f32[256,1024]{1,0:T(8,128)}, ...) | async-done | bytes 2686992 | tf_op jit(solution)/shard_map/psum | solution.py:200
  299.4 0.5 multiply_reduce_fusion.1
  299.8 21.0 %all-reduce = (f32[256]{0:T(256)S(1)}, f32[256]{0:T(256)S(1)}) all-reduce(f32[256]{0:T(256)S(1)} %get-tuple-element.9, f32[256]{0:T(256)S(1)} %get-tuple-element.7), channel_id=1, replica_groups=mesh['groups'=2,'row'=16,'col'=4,'sub'=2] {'row'}, use_global_device_ids=true, to_apply=%region_19.0 | all-reduce | flops 512 | bytes 4096 | tf_op jit(solution)/shard_map/psum | solution.py:200
  320.8 29.3 %all-reduce.2 = (f32[256]{0:T(256)}, f32[256]{0:T(256)}) all-reduce(f32[256]{0:T(256)S(1)} %get-tuple-element.13, f32[256]{0:T(256)S(1)} %get-tuple-element.14), channel_id=1, replica_groups=mesh['groups'=2,'row'=16,'col'=4,'sub'=2] {'col','sub'}, use_global_device_ids=true, to_apply=%region_20.0 | all-reduce | flops 512 | bytes 4096 | tf_op jit(solution)/shard_map/psum | solution.py:199
  350.1 0.9 add_convert_fusion.1
  351.0 33.9 %all-reduce.9.cloned.1.call-done = (f32[1024,128]{1,0:T(8,128)}, f32[256,64]{0,1:T(8,128)}, f32[256,1024]{1,0:T(8,128)}, f32[1024,256]{1,0:T(8,128)}) async-done(((f32[1024,128]{1,0:T(8,128)}, f32[256,64]{0,1:T(8,128)}, f32[256,1024]{1,0:T(8,128)}, f32[1024,256]{1,0:T(8,128)}), (f32[1024,128]{1,0:T(8,128)}, f32[256,64]{0,1:T(8,128)}, f32[256,1024]{1,0:T(8,128)}, ...) | async-done | bytes 2686992 | tf_op jit(solution)/shard_map/psum | solution.py:199
  384.9 1.9 copy.126
  386.8 1.5 copy.127
  388.3 2.3 copy.128
  390.6 2.3 copy.129
  (94 shorter events, 2.5 us)
Async XLA Ops:
  7.2 4.3 %copy-start = (bf16[256,1024]{1,0:T(8,128)(2,1)S(1)}, bf16[256,1024]{1,0:T(8,128)(2,1)}, u32[]{:S(2)}) copy-start(bf16[256,1024]{1,0:T(8,128)(2,1)} %param.17) | copy-start | bytes 1572868
  8.4 2.1 copy-start.17
  9.5 0.9 copy-start.19
  10.3 7.3 %copy-start.21 = (f32[256]{0:T(256)}, f32[256]{0:T(256)S(1)}, u32[]{:S(2)}) copy-start(f32[256]{0:T(256)S(1)} %mul.200) | copy-start | bytes 3076
  11.5 4.3 %copy-start.4 = (bf16[8,32,256]{2,1,0:T(8,128)(2,1)S(1)}, bf16[8,32,256]{2,1,0:T(8,128)(2,1)}, u32[]{:S(2)}) copy-start(bf16[8,32,256]{2,1,0:T(8,128)(2,1)} %param.11) | copy-start | bytes 393220
  11.5 4.3 %copy-start.8 = (bf16[1024,256]{1,0:T(8,128)(2,1)S(1)}, bf16[1024,256]{1,0:T(8,128)(2,1)}, u32[]{:S(2)}) copy-start(bf16[1024,256]{1,0:T(8,128)(2,1)} %param.18) | copy-start | bytes 1572868
  11.5 5.8 %copy-start.23 = (f32[256]{0:T(256)S(1)}, f32[256]{0:T(256)}, u32[]{:S(2)}) copy-start(f32[256]{0:T(256)} %param.19) | copy-start | bytes 3076
  11.5 5.9 %copy-start.10 = (bf16[256,64]{0,1:T(8,128)(2,1)S(1)}, bf16[256,64]{0,1:T(8,128)(2,1)}, u32[]{:S(2)}) copy-start(bf16[256,64]{0,1:T(8,128)(2,1)} %param.20) | copy-start | bytes 98308
  15.0 0.8 copy-start.5
  16.2 0.6 copy-start.13
  16.8 0.6 copy-start.15
  64.2 27.3 %all-to-all-start.1 = ((bf16[8,2,256]{2,1,0:T(2,128)(2,1)}), bf16[8,2,256]{2,1,0:T(2,128)(2,1)S(1)}, u32[]{:S(2)}, u32[]{:S(2)}) async-start(bf16[8,2,256]{2,1,0:T(2,128)(2,1)} %reshape.192), calls=%async_computation.1 | async-start | bytes 16384 | tf_op jit(solution)/shard_map/all_to_all | solution.py:130
  91.5 22.1 %all-to-all-start = ((bf16[8,8,2048]{2,0,1:T(8,128)(2,1)}), bf16[8,8,2048]{2,0,1:T(8,128)(2,1)}, u32[]{:S(2)}, u32[]{:S(2)}) async-start(bf16[8,8,2048]{2,0,1:T(8,128)(2,1)} %copy.49), calls=%async_computation | async-start | bytes 524288 | tf_op jit(solution)/shard_map/all_to_all | solution.py:129
  105.7 3.8 copy-start.1
  113.6 15.9 %all-to-all-start.3 = ((bf16[8,8,2048]{2,1,0:T(8,128)(2,1)}), bf16[8,8,2048]{2,1,0:T(8,128)(2,1)S(1)}, u32[]{:S(2)}, u32[]{:S(2)}) async-start(bf16[8,8,2048]{2,1,0:T(8,128)(2,1)} %convert_element_type.80), calls=%async_computation.3 | async-start | bytes 524288 | tf_op jit(solution)/shard_map/all_to_all | solution.py:165
  121.5 3.6 copy-start.2
  129.5 10.1 %all-to-all-start.2 = ((bf16[8,8,1024]{2,1,0:T(8,128)(2,1)}), bf16[8,8,1024]{2,1,0:T(8,128)(2,1)S(1)}, u32[]{:S(2)}, u32[]{:S(2)}) async-start(bf16[8,8,1024]{2,1,0:T(8,128)(2,1)} %convert_element_type.77), calls=%async_computation.2 | async-start | bytes 262144 | tf_op jit(solution)/shard_map/all_to_all | solution.py:43
  139.5 17.5 %all-to-all-start.4 = ((bf16[16,8,1024]{2,1,0:T(8,128)(2,1)}), bf16[16,8,1024]{2,1,0:T(8,128)(2,1)S(1)}, u32[]{:S(2)}, u32[]{:S(2)}) async-start(bf16[16,8,1024]{2,1,0:T(8,128)(2,1)} %copy.65), calls=%async_computation.4 | async-start | bytes 524288 | tf_op jit(solution)/shard_map/all_to_all | solution.py:43
  143.5 155.7 %all-reduce.7.cloned.1.call-start = ((), (), s32[]{:S(2)}) async-start(), calls=%async_computation.5 | async-start | bytes 5373952 | tf_op jit(solution)/shard_map/psum | solution.py:200
  143.8 2.2 copy-start.3
  148.7 2.7 copy-start.7
  152.4 4.8 %copy-start.22 = (f32[256]{0:T(256)S(1)}, f32[256]{0:T(256)}, u32[]{:S(2)}) copy-start(f32[256]{0:T(256)} %copy-done.21) | copy-start | bytes 3076
  152.4 5.8 %copy-start.11 = (bf16[256,64]{0,1:T(8,128)(2,1)S(1)}, bf16[256,64]{0,1:T(8,128)(2,1)}, u32[]{:S(2)}) copy-start(bf16[256,64]{0,1:T(8,128)(2,1)} %param.20) | copy-start | bytes 98308
  152.4 5.8 %copy-start.14 = (f32[256]{0:T(256)S(1)}, f32[256]{0:T(256)}, u32[]{:S(2)}) copy-start(f32[256]{0:T(256)} %copy-done.13) | copy-start | bytes 3076
  152.4 5.8 %copy-start.16 = (f32[256]{0:T(256)S(1)}, f32[256]{0:T(256)}, u32[]{:S(2)}) copy-start(f32[256]{0:T(256)} %copy-done.15) | copy-start | bytes 3076
  152.4 5.8 %copy-start.24 = (f32[256]{0:T(256)S(1)}, f32[256]{0:T(256)}, u32[]{:S(2)}) copy-start(f32[256]{0:T(256)} %param.19) | copy-start | bytes 3076
  152.4 6.1 %copy-start.12 = (bf16[8,32,256]{2,1,0:T(8,128)(2,1)S(1)}, bf16[8,32,256]{2,1,0:T(8,128)(2,1)}, u32[]{:S(2)}) copy-start(bf16[8,32,256]{2,1,0:T(8,128)(2,1)} %param.15) | copy-start | bytes 393220
  152.4 6.3 %copy-start.6 = (bf16[256,1024]{1,0:T(8,128)(2,1)S(1)}, bf16[256,1024]{1,0:T(8,128)(2,1)}, u32[]{:S(2)}) copy-start(bf16[256,1024]{1,0:T(8,128)(2,1)} %copy-done.5) | copy-start | bytes 1572868
  152.4 7.7 %copy-start.9 = (bf16[1024,256]{1,0:T(8,128)(2,1)S(1)}, bf16[1024,256]{1,0:T(8,128)(2,1)}, u32[]{:S(2)}) copy-start(bf16[1024,256]{1,0:T(8,128)(2,1)} %param.18) | copy-start | bytes 1572868
  162.2 137.1 %copy-start.18 = (f32[256]{0:T(256)S(1)}, f32[256]{0:T(256)}, u32[]{:S(2)}) copy-start(f32[256]{0:T(256)} %copy-done.17) | copy-start | bytes 3076
  162.2 137.1 %copy-start.20 = (f32[256]{0:T(256)S(1)}, f32[256]{0:T(256)}, u32[]{:S(2)}) copy-start(f32[256]{0:T(256)} %copy-done.19) | copy-start | bytes 3076
  162.3 137.1 %copy-start.25 = (f32[256]{0:T(256)S(1)}, f32[256]{0:T(256)}, u32[]{:S(2)}) copy-start(f32[256]{0:T(256)} %param.16) | copy-start | bytes 3076
  163.6 221.3 %all-reduce.9.cloned.1.call-start = ((), (), s32[]{:S(2)}) async-start(), calls=%async_computation.6 | async-start | bytes 5373952 | tf_op jit(solution)/shard_map/psum | solution.py:199
Sparse Core Ops, SparseCore 0:
  163.7 135.4 all-reduce.6
  301.9 82.9 all-reduce.8
